TPU v7x, 32 devices: a whole 2x2x4 slice. The times are simulated.
32 devices in a mesh: gx: 4 (over x, core), gy: 4 (over z), gz: 2 (over y).
Axes of the slice: x: 2, y: 2, z: 4, core: 2. Of those that a mesh axis runs over, the one named last changes fastest.
Arguments:
- orbitals: float32 [64, 32, 32, 256], P(None, 'gx', 'gy', 'gz'), may hold values from -6 to 6
- potential: float32 [32, 32, 256], P('gx', 'gy', 'gz'), may hold values from 0 to 0.5
- centre: float32 [64], replicated, may hold values from 3 to 5
- half_width: float32 [64], replicated, may hold values from 3 to 5
Outputs:
- filtered: float32 [64, 32, 32, 256], P(None, 'gx', 'gy', 'gz')
All inputs are finite; a program needn't handle non-finite values.
Results may differ from a plain program's by a relative error of at most 0.00002.
Values sent between devices are 32-bit elements; how exact they have to be, the bound alone decides.
A program may use at most 64 MiB of HBM per device.

v0:
```python
import jax
import jax.numpy as jnp
from jax import lax
from jax.sharding import PartitionSpec as P

shift_mass = 0.05
jacobi_weight = 2.0 / 3.0


def extended(cells, sides, width):
    for axis, dim in sides:
        count = lax.axis_size(axis)
        head = lax.slice_in_dim(cells, 0, width, axis=dim)
        tail = lax.slice_in_dim(cells, cells.shape[dim] - width, cells.shape[dim], axis=dim)
        cells = jnp.concatenate(
            [
                lax.ppermute(tail, axis, [(i, (i + 1) % count) for i in range(count)]),
                cells,
                lax.ppermute(head, axis, [((i + 1) % count, i) for i in range(count)]),
            ],
            axis=dim,
        )
    return cells


def neighbour_sum(padded):
    total = padded[:, 2:, 1:-1, 1:-1] + padded[:, :-2, 1:-1, 1:-1]
    total = total + padded[:, 1:-1, 2:, 1:-1] + padded[:, 1:-1, :-2, 1:-1]
    return total + padded[:, 1:-1, 1:-1, 2:] + padded[:, 1:-1, 1:-1, :-2]


def restrict(field):
    shape = field.shape
    return 0.5 * field.reshape(shape[0], shape[1] // 2, 2, shape[2] // 2, 2, shape[3] // 2, 2).sum(
        axis=(2, 4, 6)
    )


def average_cells(field):
    shape = field.shape
    return 0.125 * field.reshape(shape[0] // 2, 2, shape[1] // 2, 2, shape[2] // 2, 2).sum(
        axis=(1, 3, 5)
    )


def prolong(field):
    return jnp.repeat(jnp.repeat(jnp.repeat(field, 2, 1), 2, 2), 2, 3)


def relax(level, source, diagonal, coupling, extend):
    applied = diagonal * level - coupling * neighbour_sum(extend(level))
    return level + jacobi_weight * (source - applied) / diagonal


def smooth_two(source, diagonal, extend):
    level = jacobi_weight * source / diagonal
    for sweep_index in range(2):
        level = relax(level, source, diagonal, 0.03125, extend)
    return level


def level_one_rim(field):
    return extended(field, (("gx", 1), ("gy", 2), ("gz", 3)), 1)


def level_two_rim(field):
    return extended(field, (("gx", 1), ("gy", 2), ("gz", 3)), 1)


def local(orbitals, potential, centre, half_width):
    middle = centre[:, None, None, None]
    spread = half_width[:, None, None, None]
    diagonal_fine = 3.0 + potential
    widened = extended(orbitals, (("gx", 1), ("gy", 2), ("gz", 3)), 2)
    potential_wide = extended(potential, (("gx", 0), ("gy", 1), ("gz", 2)), 1)
    inner = widened[:, 1:-1, 1:-1, 1:-1]
    first_image = (3.0 + potential_wide) * inner - 0.5 * neighbour_sum(widened)
    first_wide = (first_image - middle * inner) / spread
    first_order = first_wide[:, 1:-1, 1:-1, 1:-1]
    second_image = diagonal_fine * first_order - 0.5 * neighbour_sum(first_wide)
    second_order = 2.0 * (second_image - middle * first_order) / spread - orbitals
    potential_one = average_cells(potential)
    potential_two = average_cells(potential_one)
    diagonal_one = 0.75 + potential_one + shift_mass
    source_one = restrict(second_order)
    level_one = jacobi_weight * source_one / diagonal_one
    level_one = relax(level_one, source_one, diagonal_one, 0.125, level_one_rim)
    residue = source_one - (
        diagonal_one * level_one - 0.125 * neighbour_sum(level_one_rim(level_one))
    )
    source_two = restrict(residue)
    diagonal_two = 0.1875 + potential_two + shift_mass
    level_two = smooth_two(source_two, diagonal_two, level_two_rim)
    level_one = level_one + prolong(level_two)
    level_one = relax(level_one, source_one, diagonal_one, 0.125, level_one_rim)
    return second_order + prolong(level_one)


def solution(mesh):
    in_specs = (P(None, "gx", "gy", "gz"), P("gx", "gy", "gz"), P(), P())
    out_specs = P(None, "gx", "gy", "gz")
    return jax.shard_map(local, mesh=mesh, in_specs=in_specs, out_specs=out_specs, check_vma=False)
```

profile of v0, /device:TPU:0, one launch (start us, length us, event | category | flops | bytes accessed | tf_op | source)
XLA Modules:
  0.0 225.0 jit_solution(14805342491126907157)
XLA Ops:
  7.1 3.9 %copy.13 = f32[64,8,8,128]{0,3,2,1:T(8,128)} copy(f32[64,8,8,128]{3,2,1,0:T(8,128)} %param.4) | data formatting | bytes 4194304 | tf_op args[0]
  14.9 2.4 %collective-permute-done.1 = f32[1,8,128]{2,1,0:T(8,128)S(1)} collective-permute-done((f32[1,8,128]{2,1,0:T(8,128)S(1)}, f32[1,8,128]{2,1,0:T(8,128)S(1)}, u32[]{:S(2)}, u32[]{:S(2)}) %collective-permute-start.1) | collective-permute-done | bytes 4128 | tf_op jit(solution)/shard_map/ppermute | solution.py:19
  18.0 3.6 %pad_maximum_fusion.13 = (f32[64,12,2,128]{0,3,2,1:T(8,128)}, f32[64,12,2,128]{0,3,2,1:T(8,128)}) fusion(f32[64,2,8,128]{0,3,2,1:T(8,128)S(1)} %copy.14, f32[64,8,8,128]{0,3,2,1:T(8,128)} %copy.13, f32[64,2,8,128]{0,3,2,1:T(8,128)S(1)} %copy.12), kind=kLoop, calls=%fused_computation.34 | loop fusion | flops 786432 | bytes 4718592 | tf_op jit(solution)/shard_map/slice | solution.py:14
  25.2 2.7 %copy.16 = f32[64,12,2,128]{3,0,2,1:T(8,128)} copy(f32[64,12,2,128]{0,3,2,1:T(8,128)} %get-tuple-element.8) | data formatting | bytes 1572864 | tf_op jit(solution)/shard_map/slice | solution.py:13
  30.2 3.8 %collective-permute-start.3 = (f32[10,1,128]{2,1,0:T(1,128)S(1)}, f32[10,1,128]{2,1,0:T(1,128)S(1)}, u32[]{:S(2)}, u32[]{:S(2)}) collective-permute-start(f32[10,1,128]{2,1,0:T(1,128)S(1)} %get-tuple-element.44), channel_id=1, source_target_pairs={{2,0},{4,2},{6,4},{0,6},{3,1},{5,3},{7,5},{1,7},{10,8},{12,10},{14... | collective-permute-start | bytes 15368 | tf_op jit(solution)/shard_map/ppermute | solution.py:19
  34.0 28.7 %collective-permute-done.2 = f32[10,1,128]{2,1,0:T(1,128)S(1)} collective-permute-done((f32[10,1,128]{2,1,0:T(1,128)S(1)}, f32[10,1,128]{2,1,0:T(1,128)S(1)}, u32[]{:S(2)}, u32[]{:S(2)}) %collective-permute-start.2) | collective-permute-done | bytes 5152 | tf_op jit(solution)/shard_map/ppermute | solution.py:17
  64.9 2.8 %copy.17 = f32[64,12,2,128]{0,3,2,1:T(8,128)} copy(f32[64,12,2,128]{3,0,2,1:T(8,128)} %collective-permute-done.8) | data formatting | bytes 1572864 | tf_op jit(solution)/shard_map/ppermute | solution.py:17
  67.7 2.8 %copy.18 = f32[64,12,2,128]{0,3,2,1:T(8,128)} copy(f32[64,12,2,128]{3,0,2,1:T(8,128)} %collective-permute-done.9) | data formatting | bytes 1572864 | tf_op jit(solution)/shard_map/ppermute | solution.py:19
  74.3 4.5 %collective-permute-done.10 = f32[64,12,12,2]{0,3,2,1:T(2,128)S(1)} collective-permute-done((f32[64,12,12,2]{0,3,2,1:T(2,128)S(1)}, f32[64,12,12,2]{0,3,2,1:T(2,128)S(1)}, u32[]{:S(2)}, u32[]{:S(2)}) %collective-permute-start.10) | collective-permute-done | bytes 73760 | tf_op jit(solution)/shard_map/ppermute | solution.py:17
  80.5 6.6 %pad_maximum_fusion = f32[64,12,12,132]{0,3,2,1:T(8,128)S(1)} fusion(f32[64,12,12,2]{0,3,2,1:T(2,128)S(1)} %collective-permute-done.11, f32[64,12,2,128]{0,3,2,1:T(8,128)S(1)} %copy-done.3, f32[64,2,8,128]{0,3,2,1:T(8,128)S(1)} %copy.14, f32[64,8,8,128]{0,3,2,1:T(8,128)S(1)} %copy-done, f32[64,2,8,128]{0,3,2,1:T(8,128)S(1)} %copy.12, ...), kind=kLoop, calls=%fused_computation | loop fusion | flops 7299072 | bytes 9732096 | tf_op jit(solution)/shard_map/concatenate | solution.py:15
  87.1 16.7 %fusion.4 = f32[64,10,10,130]{0,3,2,1:T(8,128)S(1)} fusion(f32[64,12,12,2]{0,3,2,1:T(2,128)S(1)} %collective-permute-done.10, f32[64,12,2,128]{0,3,2,1:T(8,128)} %copy.18, f32[64,12,2,128]{0,3,2,1:T(8,128)} %copy.17, f32[64,2,8,128]{0,3,2,1:T(8,128)S(1)} %copy.14, f32[64,8,8,128]{0,3,2,1:T(8,128)} %copy.13, f32[64,2,8,128]{0,3,2,1:T(8,128)S(1)} %copy.12, ...), kind=kLoop, calls=%fused_computation.6 | loop fusion | flops 17472000 | bytes 24886560 | tf_op jit(solution)/shard_map/div | solution.py:78
  103.9 7.5 %fusion.11 = f32[64,8,8,128]{0,3,2,1:T(8,128)} fusion(f32[64,8,8,128]{0,3,2,1:T(8,128)} %copy.13, f32[64,10,10,130]{0,3,2,1:T(8,128)S(1)} %fusion.4, f32[64]{0:T(128)S(1)} %copy-done.5, f32[64]{0:T(128)S(1)} %copy-done.6, f32[8,8,128]{2,1,0:T(8,128)S(1)} %get-tuple-element.45), kind=kLoop, calls=%fused_computation.26 | loop fusion | flops 6815744 | bytes 18907648 | tf_op jit(solution)/shard_map/sub | solution.py:81
  111.3 4.8 %reduce_sum.36 = f32[64,4,4,64]{0,3,2,1:T(8,128)S(1)} reduce(f32[64,4,2,4,2,64,2]{0,6,5,4,3,2,1:T(2,128)} %bitcast.8, f32[]{:T(128)} %constant.13.clone.1), dimensions={2,4,6}, to_apply=%region_0.0 | reduce | flops 458752 | bytes 2359300 | tf_op jit(solution)/shard_map/reduce_sum | solution.py:34
  119.2 3.0 %collective-permute-done.13 = f32[64,1,4,64]{0,3,2,1:T(8,128)S(1)} collective-permute-done((f32[64,1,4,64]{0,3,2,1:T(8,128)S(1)}, f32[64,1,4,64]{0,3,2,1:T(8,128)S(1)}, u32[]{:S(2)}, u32[]{:S(2)}) %collective-permute-start.13) | collective-permute-done | bytes 65568 | tf_op jit(solution)/shard_map/ppermute | solution.py:17
  124.3 9.1 %collective-permute-done.14 = f32[64,6,1,64]{0,3,2,1:T(8,128)S(1)} collective-permute-done((f32[64,6,1,64]{0,3,2,1:T(8,128)S(1)}, f32[64,6,1,64]{0,3,2,1:T(8,128)S(1)}, u32[]{:S(2)}, u32[]{:S(2)}) %collective-permute-start.14) | collective-permute-done | bytes 98336 | tf_op jit(solution)/shard_map/ppermute | solution.py:19
  139.9 3.2 %collective-permute-done.18 = f32[64,1,4,64]{0,3,2,1:T(8,128)S(1)} collective-permute-done((f32[64,1,4,64]{0,3,2,1:T(8,128)S(1)}, f32[64,1,4,64]{0,3,2,1:T(8,128)S(1)}, u32[]{:S(2)}, u32[]{:S(2)}) %collective-permute-start.18) | collective-permute-done | bytes 65568 | tf_op jit(solution)/shard_map/ppermute | solution.py:19
  146.4 4.4 %collective-permute-done.20 = f32[64,6,1,64]{0,3,2,1:T(8,128)S(1)} collective-permute-done((f32[64,6,1,64]{0,3,2,1:T(8,128)S(1)}, f32[64,6,1,64]{0,3,2,1:T(8,128)S(1)}, u32[]{:S(2)}, u32[]{:S(2)}) %collective-permute-start.20) | collective-permute-done | bytes 98336 | tf_op jit(solution)/shard_map/ppermute | solution.py:19
  150.7 4.6 %collective-permute-done.21 = f32[64,6,1,64]{0,3,2,1:T(8,128)S(1)} collective-permute-done((f32[64,6,1,64]{0,3,2,1:T(8,128)S(1)}, f32[64,6,1,64]{0,3,2,1:T(8,128)S(1)}, u32[]{:S(2)}, u32[]{:S(2)}) %collective-permute-start.21) | collective-permute-done | bytes 98336 | tf_op jit(solution)/shard_map/ppermute | solution.py:17
  162.0 2.7 %collective-permute-done.25 = f32[64,1,2,32]{0,3,2,1:T(8,128)S(1)} collective-permute-done((f32[64,1,2,32]{0,3,2,1:T(8,128)S(1)}, f32[64,1,2,32]{0,3,2,1:T(8,128)S(1)}, u32[]{:S(2)}, u32[]{:S(2)}) %collective-permute-start.25) | collective-permute-done | bytes 16416 | tf_op jit(solution)/shard_map/ppermute | solution.py:17
  169.1 3.5 %collective-permute-done.27 = f32[64,4,1,32]{0,3,2,1:T(8,128)S(1)} collective-permute-done((f32[64,4,1,32]{0,3,2,1:T(8,128)S(1)}, f32[64,4,1,32]{0,3,2,1:T(8,128)S(1)}, u32[]{:S(2)}, u32[]{:S(2)}) %collective-permute-start.27) | collective-permute-done | bytes 32800 | tf_op jit(solution)/shard_map/ppermute | solution.py:17
  193.4 2.9 %collective-permute-done.36 = f32[64,1,4,64]{0,3,2,1:T(8,128)S(1)} collective-permute-done((f32[64,1,4,64]{0,3,2,1:T(8,128)S(1)}, f32[64,1,4,64]{0,3,2,1:T(8,128)S(1)}, u32[]{:S(2)}, u32[]{:S(2)}) %collective-permute-start.36) | collective-permute-done | bytes 65568 | tf_op jit(solution)/shard_map/ppermute | solution.py:19
  200.4 8.6 %collective-permute-done.38 = f32[64,6,1,64]{0,3,2,1:T(8,128)S(1)} collective-permute-done((f32[64,6,1,64]{0,3,2,1:T(8,128)S(1)}, f32[64,6,1,64]{0,3,2,1:T(8,128)S(1)}, u32[]{:S(2)}, u32[]{:S(2)}) %collective-permute-start.38) | collective-permute-done | bytes 98336 | tf_op jit(solution)/shard_map/ppermute | solution.py:19
  217.7 3.2 %copy_add_fusion = f32[64,8,8,128]{0,3,2,1:T(8,128)} fusion(f32[64,8,8,128]{0,3,2,1:T(8,128)S(1)} %copy-done.1, f32[64,8,8,128]{0,2,3,1:T(8,128)S(1)} %bitcast.9), kind=kLoop, calls=%fused_computation.31 | loop fusion | flops 524288 | bytes 6291456 | tf_op jit(solution)/shard_map/add | solution.py:96
  220.9 4.2 %copy.22 = f32[64,8,8,128]{3,2,1,0:T(8,128)} copy(f32[64,8,8,128]{0,3,2,1:T(8,128)} %copy_add_fusion) | data formatting | bytes 4194304 | tf_op jit(solution)/shard_map/add | solution.py:96
  (137 shorter events, 84.4 us)
Async XLA Ops:
  2.3 15.0 %collective-permute-start.6 = (f32[64,2,8,128]{3,2,1,0:T(8,128)}, f32[64,2,8,128]{3,2,1,0:T(8,128)S(1)}, u32[]{:S(2)}, u32[]{:S(2)}) collective-permute-start(f32[64,2,8,128]{3,2,1,0:T(8,128)} %get-tuple-element.9), channel_id=1, source_target_pairs={{0,8},{8,16},{16,24},{24,0},{1,9},{9,17},{17,25},{25,1},{2,10},{10... | collective-permute-start | bytes 1572872 | tf_op jit(solution)/shard_map/ppermute | solution.py:17
  2.8 14.9 %collective-permute-start.7 = (f32[64,2,8,128]{3,2,1,0:T(8,128)}, f32[64,2,8,128]{3,2,1,0:T(8,128)S(1)}, u32[]{:S(2)}, u32[]{:S(2)}) collective-permute-start(f32[64,2,8,128]{3,2,1,0:T(8,128)} %get-tuple-element.10), channel_id=1, source_target_pairs={{8,0},{16,8},{24,16},{0,24},{9,1},{17,9},{25,17},{1,25},{10,2},{18... | collective-permute-start | bytes 1572872 | tf_op jit(solution)/shard_map/ppermute | solution.py:19
  5.4 9.5 %collective-permute-start = (f32[1,8,128]{2,1,0:T(8,128)S(1)}, f32[1,8,128]{2,1,0:T(8,128)S(1)}, u32[]{:S(2)}, u32[]{:S(2)}) collective-permute-start(f32[1,8,128]{2,1,0:T(8,128)S(1)} %get-tuple-element.48), channel_id=1, source_target_pairs={{0,8},{8,16},{16,24},{24,0},{1,9},{9,17},{17,25},{25,1},{2,10},{10... | collective-permute-start | bytes 12296 | tf_op jit(solution)/shard_map/ppermute | solution.py:17
  6.1 11.3 %collective-permute-start.1 = (f32[1,8,128]{2,1,0:T(8,128)S(1)}, f32[1,8,128]{2,1,0:T(8,128)S(1)}, u32[]{:S(2)}, u32[]{:S(2)}) collective-permute-start(f32[1,8,128]{2,1,0:T(8,128)S(1)} %get-tuple-element.47), channel_id=1, source_target_pairs={{8,0},{16,8},{24,16},{0,24},{9,1},{17,9},{25,17},{1,25},{10,2},{18... | collective-permute-start | bytes 12296 | tf_op jit(solution)/shard_map/ppermute | solution.py:19
  23.5 41.4 %collective-permute-start.8 = (f32[64,12,2,128]{3,0,2,1:T(8,128)S(1)}, f32[64,12,2,128]{3,0,2,1:T(8,128)}, u32[]{:S(2)}, u32[]{:S(2)}) collective-permute-start(f32[64,12,2,128]{3,0,2,1:T(8,128)S(1)} %copy.15), channel_id=1, source_target_pairs={{0,2},{2,4},{4,6},{6,0},{1,3},{3,5},{5,7},{7,1},{8,10},{10,12},{12... | collective-permute-start | bytes 2359304 | tf_op jit(solution)/shard_map/ppermute | solution.py:17
  27.9 39.8 %collective-permute-start.9 = (f32[64,12,2,128]{3,0,2,1:T(8,128)}, f32[64,12,2,128]{3,0,2,1:T(8,128)}, u32[]{:S(2)}, u32[]{:S(2)}) collective-permute-start(f32[64,12,2,128]{3,0,2,1:T(8,128)} %copy.16), channel_id=1, source_target_pairs={{2,0},{4,2},{6,4},{0,6},{3,1},{5,3},{7,5},{1,7},{10,8},{12,10},{14... | collective-permute-start | bytes 2359304 | tf_op jit(solution)/shard_map/ppermute | solution.py:19
  30.1 32.6 %collective-permute-start.2 = (f32[10,1,128]{2,1,0:T(1,128)S(1)}, f32[10,1,128]{2,1,0:T(1,128)S(1)}, u32[]{:S(2)}, u32[]{:S(2)}) collective-permute-start(f32[10,1,128]{2,1,0:T(1,128)S(1)} %get-tuple-element.43), channel_id=1, source_target_pairs={{0,2},{2,4},{4,6},{6,0},{1,3},{3,5},{5,7},{7,1},{8,10},{10,12},{12... | collective-permute-start | bytes 15368 | tf_op jit(solution)/shard_map/ppermute | solution.py:17
  30.2 32.5 %collective-permute-start.3 = (f32[10,1,128]{2,1,0:T(1,128)S(1)}, f32[10,1,128]{2,1,0:T(1,128)S(1)}, u32[]{:S(2)}, u32[]{:S(2)}) collective-permute-start(f32[10,1,128]{2,1,0:T(1,128)S(1)} %get-tuple-element.44), channel_id=1, source_target_pairs={{2,0},{4,2},{6,4},{0,6},{3,1},{5,3},{7,5},{1,7},{10,8},{12,10},{14... | collective-permute-start | bytes 15368 | tf_op jit(solution)/shard_map/ppermute | solution.py:19
  62.8 11.3 %collective-permute-start.4 = (f32[10,10,1]{2,1,0:T(8,128)S(1)}, f32[10,10,1]{2,1,0:T(8,128)S(1)}, u32[]{:S(2)}, u32[]{:S(2)}) collective-permute-start(f32[10,10,1]{2,1,0:T(8,128)S(1)} %get-tuple-element.37), channel_id=1, source_target_pairs={{0,1},{1,0},{2,3},{3,2},{4,5},{5,4},{6,7},{7,6},{8,9},{9,8},{10,11... | collective-permute-start | bytes 1208 | tf_op jit(solution)/shard_map/ppermute | solution.py:17
  64.4 9.7 %collective-permute-start.5 = (f32[10,10,1]{2,1,0:T(8,128)S(1)}, f32[10,10,1]{2,1,0:T(8,128)S(1)}, u32[]{:S(2)}, u32[]{:S(2)}) collective-permute-start(f32[10,10,1]{2,1,0:T(8,128)S(1)} %get-tuple-element.38), channel_id=1, source_target_pairs={{1,0},{0,1},{3,2},{2,3},{5,4},{4,5},{7,6},{6,7},{9,8},{8,9},{11,10... | collective-permute-start | bytes 1208 | tf_op jit(solution)/shard_map/ppermute | solution.py:19
  72.0 6.8 %collective-permute-start.10 = (f32[64,12,12,2]{0,3,2,1:T(2,128)S(1)}, f32[64,12,12,2]{0,3,2,1:T(2,128)S(1)}, u32[]{:S(2)}, u32[]{:S(2)}) collective-permute-start(f32[64,12,12,2]{0,3,2,1:T(2,128)S(1)} %get-tuple-element.6), channel_id=1, source_target_pairs={{0,1},{1,0},{2,3},{3,2},{4,5},{5,4},{6,7},{7,6},{8,9},{9,8},{10,11... | collective-permute-start | bytes 221192 | tf_op jit(solution)/shard_map/ppermute | solution.py:17
  73.6 6.9 %collective-permute-start.11 = (f32[64,12,12,2]{0,3,2,1:T(2,128)S(1)}, f32[64,12,12,2]{0,3,2,1:T(2,128)S(1)}, u32[]{:S(2)}, u32[]{:S(2)}) collective-permute-start(f32[64,12,12,2]{0,3,2,1:T(2,128)S(1)} %get-tuple-element.5), channel_id=1, source_target_pairs={{1,0},{0,1},{3,2},{2,3},{5,4},{4,5},{7,6},{6,7},{9,8},{8,9},{11,10... | collective-permute-start | bytes 221192 | tf_op jit(solution)/shard_map/ppermute | solution.py:19
  116.5 5.7 %collective-permute-start.13 = (f32[64,1,4,64]{0,3,2,1:T(8,128)S(1)}, f32[64,1,4,64]{0,3,2,1:T(8,128)S(1)}, u32[]{:S(2)}, u32[]{:S(2)}) collective-permute-start(f32[64,1,4,64]{0,3,2,1:T(8,128)S(1)} %get-tuple-element.27), channel_id=1, source_target_pairs={{0,8},{8,16},{16,24},{24,0},{1,9},{9,17},{17,25},{25,1},{2,10},{10... | collective-permute-start | bytes 196616 | tf_op jit(solution)/shard_map/ppermute | solution.py:17
  122.2 11.2 %collective-permute-start.14 = (f32[64,6,1,64]{0,3,2,1:T(8,128)S(1)}, f32[64,6,1,64]{0,3,2,1:T(8,128)S(1)}, u32[]{:S(2)}, u32[]{:S(2)}) collective-permute-start(f32[64,6,1,64]{0,3,2,1:T(8,128)S(1)} %get-tuple-element.22), channel_id=1, source_target_pairs={{2,0},{4,2},{6,4},{0,6},{3,1},{5,3},{7,5},{1,7},{10,8},{12,10},{14... | collective-permute-start | bytes 294920 | tf_op jit(solution)/shard_map/ppermute | solution.py:19
  123.7 9.7 %collective-permute-start.15 = (f32[64,6,1,64]{0,3,2,1:T(8,128)S(1)}, f32[64,6,1,64]{0,3,2,1:T(8,128)S(1)}, u32[]{:S(2)}, u32[]{:S(2)}) collective-permute-start(f32[64,6,1,64]{0,3,2,1:T(8,128)S(1)} %get-tuple-element.21), channel_id=1, source_target_pairs={{0,2},{2,4},{4,6},{6,0},{1,3},{3,5},{5,7},{7,1},{8,10},{10,12},{12... | collective-permute-start | bytes 294920 | tf_op jit(solution)/shard_map/ppermute | solution.py:17
  139.4 4.4 %collective-permute-start.19 = (f32[64,1,4,64]{0,3,2,1:T(8,128)S(1)}, f32[64,1,4,64]{0,3,2,1:T(8,128)S(1)}, u32[]{:S(2)}, u32[]{:S(2)}) collective-permute-start(f32[64,1,4,64]{0,3,2,1:T(8,128)S(1)} %get-tuple-element.25), channel_id=1, source_target_pairs={{0,8},{8,16},{16,24},{24,0},{1,9},{9,17},{17,25},{25,1},{2,10},{10... | collective-permute-start | bytes 196616 | tf_op jit(solution)/shard_map/ppermute | solution.py:17
  143.9 6.8 %collective-permute-start.20 = (f32[64,6,1,64]{0,3,2,1:T(8,128)S(1)}, f32[64,6,1,64]{0,3,2,1:T(8,128)S(1)}, u32[]{:S(2)}, u32[]{:S(2)}) collective-permute-start(f32[64,6,1,64]{0,3,2,1:T(8,128)S(1)} %get-tuple-element.20), channel_id=1, source_target_pairs={{2,0},{4,2},{6,4},{0,6},{3,1},{5,3},{7,5},{1,7},{10,8},{12,10},{14... | collective-permute-start | bytes 294920 | tf_op jit(solution)/shard_map/ppermute | solution.py:19
  145.4 9.9 %collective-permute-start.21 = (f32[64,6,1,64]{0,3,2,1:T(8,128)S(1)}, f32[64,6,1,64]{0,3,2,1:T(8,128)S(1)}, u32[]{:S(2)}, u32[]{:S(2)}) collective-permute-start(f32[64,6,1,64]{0,3,2,1:T(8,128)S(1)} %get-tuple-element.19), channel_id=1, source_target_pairs={{0,2},{2,4},{4,6},{6,0},{1,3},{3,5},{5,7},{7,1},{8,10},{10,12},{12... | collective-permute-start | bytes 294920 | tf_op jit(solution)/shard_map/ppermute | solution.py:17
  160.4 4.3 %collective-permute-start.25 = (f32[64,1,2,32]{0,3,2,1:T(8,128)S(1)}, f32[64,1,2,32]{0,3,2,1:T(8,128)S(1)}, u32[]{:S(2)}, u32[]{:S(2)}) collective-permute-start(f32[64,1,2,32]{0,3,2,1:T(8,128)S(1)} %get-tuple-element.41), channel_id=1, source_target_pairs={{0,8},{8,16},{16,24},{24,0},{1,9},{9,17},{17,25},{25,1},{2,10},{10... | collective-permute-start | bytes 49160 | tf_op jit(solution)/shard_map/ppermute | solution.py:17
  166.6 6.1 %collective-permute-start.27 = (f32[64,4,1,32]{0,3,2,1:T(8,128)S(1)}, f32[64,4,1,32]{0,3,2,1:T(8,128)S(1)}, u32[]{:S(2)}, u32[]{:S(2)}) collective-permute-start(f32[64,4,1,32]{0,3,2,1:T(8,128)S(1)} %get-tuple-element.35), channel_id=1, source_target_pairs={{0,2},{2,4},{4,6},{6,0},{1,3},{3,5},{5,7},{7,1},{8,10},{10,12},{12... | collective-permute-start | bytes 98312 | tf_op jit(solution)/shard_map/ppermute | solution.py:17
  182.3 6.1 %collective-permute-start.33 = (f32[64,4,1,32]{0,3,2,1:T(8,128)S(1)}, f32[64,4,1,32]{0,3,2,1:T(8,128)S(1)}, u32[]{:S(2)}, u32[]{:S(2)}) collective-permute-start(f32[64,4,1,32]{0,3,2,1:T(8,128)S(1)} %get-tuple-element.33), channel_id=1, source_target_pairs={{0,2},{2,4},{4,6},{6,0},{1,3},{3,5},{5,7},{7,1},{8,10},{10,12},{12... | collective-permute-start | bytes 98312 | tf_op jit(solution)/shard_map/ppermute | solution.py:17
  192.9 5.4 %collective-permute-start.37 = (f32[64,1,4,64]{0,3,2,1:T(8,128)S(1)}, f32[64,1,4,64]{0,3,2,1:T(8,128)S(1)}, u32[]{:S(2)}, u32[]{:S(2)}) collective-permute-start(f32[64,1,4,64]{0,3,2,1:T(8,128)S(1)} %get-tuple-element.23), channel_id=1, source_target_pairs={{0,8},{8,16},{16,24},{24,0},{1,9},{9,17},{17,25},{25,1},{2,10},{10... | collective-permute-start | bytes 196616 | tf_op jit(solution)/shard_map/ppermute | solution.py:17
  198.4 10.7 %collective-permute-start.38 = (f32[64,6,1,64]{0,3,2,1:T(8,128)S(1)}, f32[64,6,1,64]{0,3,2,1:T(8,128)S(1)}, u32[]{:S(2)}, u32[]{:S(2)}) collective-permute-start(f32[64,6,1,64]{0,3,2,1:T(8,128)S(1)} %get-tuple-element.18), channel_id=1, source_target_pairs={{2,0},{4,2},{6,4},{0,6},{3,1},{5,3},{7,5},{1,7},{10,8},{12,10},{14... | collective-permute-start | bytes 294920 | tf_op jit(solution)/shard_map/ppermute | solution.py:19
  198.7 10.3 %collective-permute-start.39 = (f32[64,6,1,64]{0,3,2,1:T(8,128)S(1)}, f32[64,6,1,64]{0,3,2,1:T(8,128)S(1)}, u32[]{:S(2)}, u32[]{:S(2)}) collective-permute-start(f32[64,6,1,64]{0,3,2,1:T(8,128)S(1)} %get-tuple-element.17), channel_id=1, source_target_pairs={{0,2},{2,4},{4,6},{6,0},{1,3},{3,5},{5,7},{7,1},{8,10},{10,12},{12... | collective-permute-start | bytes 294920 | tf_op jit(solution)/shard_map/ppermute | solution.py:17
  (25 other events, 132.1 us)
where the time goes:
time: 226 us; the launch traced here: 225 us
  waiting for transfers between devices  111 us (49%)
  other arithmetic  46.7 us (21%)
  starting transfers between devices  39.7 us (18%)
  local copies, waits for them, and re-layouts  27.3 us (12%)
    ppermute x21, waiting for transfers between devices, extended(): lax.ppermute(tail, axis, [(i, (i + 1) % count) for i in range(count)])  61.2 us
    ppermute x21, waiting for transfers between devices, extended(): lax.ppermute(head, axis, [((i + 1) % count, i) for i in range(count)])  49.7 us
    ppermute x21, starting transfers between devices, extended(): lax.ppermute(head, axis, [((i + 1) % count, i) for i in range(count)])  21.9 us
    ppermute x21, starting transfers between devices, extended(): lax.ppermute(tail, axis, [(i, (i + 1) % count) for i in range(count)])  17.8 us
    div x1, other arithmetic, local(): first_wide = (first_image - middle * inner) / spread  16.7 us
    concatenate x8, other arithmetic, extended(): jnp.concatenate([lax.ppermute(tail, axis, [(i, (i + 1) % count) for i in...  8.22 us
    sub x1, other arithmetic, local(): 2.0 * (second_image - middle * first_order) / spread - orbitals  7.46 us
    reduce_sum x2, other arithmetic, restrict(): field.reshape(shape[0], shape[1] // 2, 2, shape[2] // 2, 2, shape[3] // 2...  5.15 us
  transfers between devices with their start and end apart: 42, of which 33 were waited for; matrix products, arithmetic and copies ran while one was open for 8% of the time, Pallas kernels for 0%

commit v1 on v0

v1 whole, which is shorter than its diff:
```python
import functools

import jax
import jax.numpy as jnp
from jax import lax
from jax.experimental import pallas as pl
from jax.experimental.pallas import tpu as pltpu
from jax.sharding import PartitionSpec as P

shift_mass = 0.05
jacobi_weight = 2.0 / 3.0
MESH = pl.DeviceIdType.MESH
ORB, FIRST, LEV_A, LEV_B, TWO_A, TWO_B, TWO_C = range(7)


def kernel(sizes, chunks, centre, half_width, pot, orbitals, out, *scratch):
    ext = scratch[0:7]
    second, zsend, zrecv, band_a, band_i, pot_b, d1_b, r1_b, r2_b = scratch[7:16]
    load_sem, store_sem, send_sem, recv_sem = scratch[16:20]
    bands, nx, ny, nz = second.shape[2], second.shape[0], second.shape[1], second.shape[3]
    width = bands // chunks
    groups = width // 8
    two_sided = sizes["gz"] > 2
    dims = [(nx, ny, 1)] * 2 + [(nx // 2, ny // 2, 2)] * 2 + [(nx // 4, ny // 4, 4)] * 3
    lane = lax.broadcasted_iota(jnp.int32, (8, nz), 1)
    sub = lax.broadcasted_iota(jnp.int32, (8, nz), 0)

    near = {}
    for axis in ("gx", "gy", "gz"):
        me, n = lax.axis_index(axis), sizes[axis]
        near[axis] = ({axis: lax.rem(me + n - 1, n)}, {axis: lax.rem(me + 1, n)})
    peers = [near["gx"][0], near["gx"][1], near["gy"][0], near["gy"][1], near["gz"][1]]
    if two_sided:
        peers.append(near["gz"][0])

    def loads(k):
        rows = pl.ds(pl.multiple_of(k * width, 8), width)

        def line(x, _):
            for y in range(ny):
                pltpu.make_async_copy(
                    orbitals.at[rows, x, y], ext[ORB].at[x + 1, y + 1, rows], load_sem.at[k]
                ).start()
            return 0

        lax.fori_loop(0, nx, line, 0)

    lax.fori_loop(0, chunks, lambda k, c: (loads(k), c)[1], 0)

    barrier = pltpu.get_barrier_semaphore()
    for peer in peers:
        pl.semaphore_signal(barrier, inc=1, device_id=peer, device_id_type=MESH)

    def copies(p, k):
        mx, my, _ = dims[p]
        e = ext[p]
        rows = pl.ds(pl.multiple_of(k * width, 8), width)
        ys, xs = pl.ds(1, my), pl.ds(1, mx)
        moves = [
            (e.at[1, ys, rows], e.at[mx + 1, ys, rows], near["gx"][0]),
            (e.at[mx, ys, rows], e.at[0, ys, rows], near["gx"][1]),
            (e.at[xs, 1, rows], e.at[xs, my + 1, rows], near["gy"][0]),
            (e.at[xs, my, rows], e.at[xs, 0, rows], near["gy"][1]),
            (zsend.at[p, rows], zrecv.at[p, 0, rows], near["gz"][1]),
        ]
        if two_sided:
            moves.append((zsend.at[p, rows], zrecv.at[p, 1, rows], near["gz"][0]))
        return [
            pltpu.make_async_remote_copy(
                src_ref=src,
                dst_ref=dst,
                send_sem=send_sem.at[p, k, j],
                recv_sem=recv_sem.at[p, k, j],
                device_id=to,
                device_id_type=MESH,
            )
            for j, (src, dst, to) in enumerate(moves)
        ]

    def send(p, k):
        for copy in copies(p, k):
            copy.start()

    def receive(p, k):
        for copy in copies(p, k):
            copy.wait_recv()

    def roll(v, shift):
        return pltpu.roll(v, shift % nz, v.ndim - 1)

    def pack(p, get):
        mx, my, w = dims[p]
        acc = jnp.zeros((8, nz), jnp.float32)
        for x in range(mx):
            for y in range(my):
                at = 2 * w * (x * my + y)
                here = (lane >= at) & (lane < at + 2 * w)
                acc = jnp.where(here, roll(get(x, y), at + w), acc)
        return acc

    def pack_store(p, sl):
        zsend[p, sl] = pack(p, lambda x, y: ext[p][x + 1, y + 1, sl])

    def edges(p, sl):
        w = dims[p][2]
        got = zrecv[p, 0, sl]
        if two_sided:
            got = jnp.where(lax.rem(lane, 2 * w) < w, got, zrecv[p, 1, sl])
        return got

    def edge_at(p, got, x, y):
        _, my, w = dims[p]
        return roll(got, -(2 * w * (x * my + y)) - w)

    def along_z(v, h, w):
        low = roll(jnp.where(lane[None] >= nz - w, h, v), w)
        high = roll(jnp.where(lane[None] < w, h, v), -w)
        return low + high

    def around(p, sl, got, x):
        _, my, w = dims[p]
        e = ext[p]
        c = e[x + 1, pl.ds(1, my), sl]
        total = e[x, pl.ds(1, my), sl] + e[x + 2, pl.ds(1, my), sl]
        total = total + (e[x + 1, pl.ds(0, my), sl] + e[x + 1, pl.ds(2, my), sl])
        h = jnp.stack([edge_at(p, got, x, y) for y in range(my)])
        return c, total + along_z(c, h, w)

    def pair_sum(v, w):
        even = lax.rem(lane, 2 * w) < w
        return v + jnp.where(even, roll(v, -w), roll(v, w))

    def each(body, p_in, p_out):
        def one(k, carry):
            if p_in is not None:
                receive(p_in, k)
            for gg in range(groups) if groups == 1 else [None]:
                if gg is None:
                    def inner(i, c):
                        body(pl.ds(pl.multiple_of(k * width + i * 8, 8), 8))
                        return c
                    lax.fori_loop(0, groups, inner, 0)
                else:
                    body(pl.ds(pl.multiple_of(k * width, 8), 8))
            if p_out is not None:
                send(p_out, k)
            return carry

        lax.fori_loop(0, chunks, one, 0)

    for g in range(bands // 8):
        m = jnp.zeros((8, nz), jnp.float32)
        s = jnp.ones((8, nz), jnp.float32)
        for j in range(8):
            m = jnp.where(sub == j, centre[g * 8 + j], m)
            s = jnp.where(sub == j, half_width[g * 8 + j], s)
        band_a[pl.ds(g * 8, 8)] = 3.0 - m
        band_i[pl.ds(g * 8, 8)] = 1.0 / s
    for x in range(nx):
        for y in range(ny):
            pot_b[x, y] = jnp.broadcast_to(pot[x, pl.ds(y, 1), :], (8, nz))
    for qx in range(nx // 4):
        for qy in range(ny // 4):
            quad = jnp.zeros((8, nz), jnp.float32)
            for hx in range(2):
                for hy in range(2):
                    x, y = 2 * qx + hx, 2 * qy + hy
                    v = pot_b[2 * x, 2 * y] + pot_b[2 * x + 1, 2 * y]
                    v = v + (pot_b[2 * x, 2 * y + 1] + pot_b[2 * x + 1, 2 * y + 1])
                    one = 0.125 * pair_sum(v, 1)
                    quad = quad + one
                    d1 = 0.75 + one + shift_mass
                    d1_b[x, y] = d1
                    r1_b[x, y] = jacobi_weight / d1
            r2_b[qx, qy] = jacobi_weight / (0.1875 + 0.125 * pair_sum(quad, 2) + shift_mass)

    pl.semaphore_wait(barrier, len(peers))

    def start(k, carry):
        rows = pl.ds(pl.multiple_of(k * width, 8), width)
        whole = ext[ORB].at[pl.ds(1, nx), pl.ds(1, ny), rows]
        pltpu.make_async_copy(whole, whole, load_sem.at[k]).wait()

        def inner(i, c):
            pack_store(ORB, pl.ds(pl.multiple_of(k * width + i * 8, 8), 8))
            return c

        lax.fori_loop(0, groups, inner, 0)
        send(ORB, k)
        return carry

    lax.fori_loop(0, chunks, start, 0)

    def step_first(sl):
        got = edges(ORB, sl)
        a, i = band_a[sl], band_i[sl]
        for x in range(nx):
            c, total = around(ORB, sl, got, x)
            ext[FIRST][x + 1, pl.ds(1, ny), sl] = ((pot_b[x] + a) * c - 0.5 * total) * i
        pack_store(FIRST, sl)

    each(step_first, ORB, FIRST)

    def step_second(sl):
        got = edges(FIRST, sl)
        a, i = band_a[sl], 2.0 * band_i[sl]
        for x2 in range(nx // 2):
            pair = None
            for x in (2 * x2, 2 * x2 + 1):
                c, total = around(FIRST, sl, got, x)
                v = ((pot_b[x] + a) * c - 0.5 * total) * i - ext[ORB][x + 1, pl.ds(1, ny), sl]
                second[x, :, sl] = v
                pair = v if pair is None else pair + v
            for y2 in range(ny // 2):
                s = 0.5 * pair_sum(pair[2 * y2] + pair[2 * y2 + 1], 1)
                ext[LEV_A][x2 + 1, y2 + 1, sl] = r1_b[x2, y2] * s
        pack_store(LEV_A, sl)

    each(step_second, FIRST, LEV_A)

    def step_level(sl):
        got = edges(LEV_A, sl)
        for x in range(nx // 2):
            c, total = around(LEV_A, sl, got, x)
            ext[LEV_B][x + 1, pl.ds(1, ny // 2), sl] = (
                (2.0 - jacobi_weight) * c + 0.125 * r1_b[x] * total
            )
        pack_store(LEV_B, sl)

    each(step_level, LEV_A, LEV_B)

    def step_residue(sl):
        got = edges(LEV_B, sl)
        for x2 in range(nx // 4):
            pair = None
            for x in (2 * x2, 2 * x2 + 1):
                c, total = around(LEV_B, sl, got, x)
                d = d1_b[x]
                source = ext[LEV_A][x + 1, pl.ds(1, ny // 2), sl] * (d * (1.0 / jacobi_weight))
                v = source - d * c + 0.125 * total
                pair = v if pair is None else pair + v
            for y2 in range(ny // 4):
                s = 0.5 * pair_sum(pair[2 * y2] + pair[2 * y2 + 1], 2)
                ext[TWO_A][x2 + 1, y2 + 1, sl] = r2_b[x2, y2] * s
        pack_store(TWO_A, sl)

    each(step_residue, LEV_B, TWO_A)

    def step_two(sl):
        got = edges(TWO_A, sl)
        for x in range(nx // 4):
            c, total = around(TWO_A, sl, got, x)
            ext[TWO_B][x + 1, pl.ds(1, ny // 4), sl] = (
                (2.0 - jacobi_weight) * c + 0.03125 * r2_b[x] * total
            )
        pack_store(TWO_B, sl)

    each(step_two, TWO_A, TWO_B)

    def step_two_again(sl):
        got = edges(TWO_B, sl)
        for x in range(nx // 4):
            c, total = around(TWO_B, sl, got, x)
            scaled = ext[TWO_A][x + 1, pl.ds(1, ny // 4), sl]
            ext[TWO_C][x + 1, pl.ds(1, ny // 4), sl] = (
                (1.0 - jacobi_weight) * c + scaled + 0.03125 * r2_b[x] * total
            )
        pack_store(TWO_C, sl)

    each(step_two_again, TWO_B, TWO_C)

    def step_last(sl):
        hx, hy = nx // 2, ny // 2
        fine, coarse = ext[LEV_B], ext[TWO_C]

        def at(x, y):
            return fine[x + 1, y + 1, sl] + coarse[(x + 2) // 2, (y + 2) // 2, sl]

        got_one, got_two = edges(LEV_B, sl), edges(TWO_C, sl)
        for x in range(hx):
            for y in range(hy):
                c = at(x, y)
                total = (at(x - 1, y) + at(x + 1, y)) + (at(x, y - 1) + at(x, y + 1))
                h = edge_at(LEV_B, got_one, x, y) + edge_at(TWO_C, got_two, x // 2, y // 2)
                total = total + along_z(c[None], h[None], 2)[0]
                v = (1.0 - jacobi_weight) * c + ext[LEV_A][x + 1, y + 1, sl]
                v = v + 0.125 * r1_b[x, y] * total
                for i in range(2):
                    for j in range(2):
                        fx, fy = 2 * x + i, 2 * y + j
                        second[fx, fy, sl] = second[fx, fy, sl] + v

    def finish(k, carry):
        rows = pl.ds(pl.multiple_of(k * width, 8), width)
        receive(TWO_C, k)

        def inner(i, c):
            step_last(pl.ds(pl.multiple_of(k * width + i * 8, 8), 8))
            return c

        lax.fori_loop(0, groups, inner, 0)

        def line(x, c):
            for y in range(ny):
                pltpu.make_async_copy(
                    second.at[x, y, rows], out.at[rows, x, y], store_sem.at[k]
                ).start()
            return c

        lax.fori_loop(0, nx, line, 0)
        return carry

    lax.fori_loop(0, chunks, finish, 0)

    def drain(k, carry):
        rows = pl.ds(pl.multiple_of(k * width, 8), width)
        for p in range(7):
            for copy in copies(p, k):
                copy.wait_send()
        whole = second.at[:, :, rows]
        pltpu.make_async_copy(whole, whole, store_sem.at[k]).wait()
        return carry

    lax.fori_loop(0, chunks, drain, 0)


def local(sizes, chunks, orbitals, potential, centre, half_width):
    bands, nx, ny, nz = orbitals.shape

    def f32(*shape):
        return pltpu.VMEM(shape, jnp.float32)

    def padded(cut):
        return f32(nx // cut + 2, ny // cut + 2, bands, nz)

    scratch = [padded(1)] * 2 + [padded(2)] * 2 + [padded(4)] * 3
    scratch += [
        f32(nx, ny, bands, nz),
        f32(7, bands, nz),
        f32(7, 2, bands, nz),
        f32(bands, nz),
        f32(bands, nz),
        f32(nx, ny, 8, nz),
        f32(nx // 2, ny // 2, 8, nz),
        f32(nx // 2, ny // 2, 8, nz),
        f32(nx // 4, ny // 4, 8, nz),
        pltpu.SemaphoreType.DMA((chunks,)),
        pltpu.SemaphoreType.DMA((chunks,)),
        pltpu.SemaphoreType.DMA((7, chunks, 6)),
        pltpu.SemaphoreType.DMA((7, chunks, 6)),
    ]
    return pl.pallas_call(
        functools.partial(kernel, sizes, chunks),
        out_shape=jax.ShapeDtypeStruct(orbitals.shape, jnp.float32),
        in_specs=[
            pl.BlockSpec(memory_space=pltpu.SMEM),
            pl.BlockSpec(memory_space=pltpu.SMEM),
            pl.BlockSpec(memory_space=pltpu.VMEM),
            pl.BlockSpec(memory_space=pl.ANY),
        ],
        out_specs=pl.BlockSpec(memory_space=pl.ANY),
        scratch_shapes=scratch,
        compiler_params=pltpu.CompilerParams(
            collective_id=0, has_side_effects=True, vmem_limit_bytes=48 * 1024 * 1024
        ),
    )(centre, half_width, potential, orbitals)


def solution(mesh):
    in_specs = (P(None, "gx", "gy", "gz"), P("gx", "gy", "gz"), P(), P())
    out_specs = P(None, "gx", "gy", "gz")
    body = functools.partial(local, dict(mesh.shape), 4)
    return jax.shard_map(body, mesh=mesh, in_specs=in_specs, out_specs=out_specs, check_vma=False)
```

time: 226 us -> 67.2 us (0.30)
  waiting for transfers between devices: 111 us -> 0 us
  Pallas kernels: 0 us -> 62 us
  other arithmetic: 46.7 us -> 0 us
  starting transfers between devices: 39.7 us -> 0 us
  local copies, waits for them, and re-layouts: 27.3 us -> 4.98 us
    ppermute x42 -> x0, waiting for transfers between devices: 111 us -> none  [the longest x21 61.2 us: extended(): lax.ppermute(tail, axis, [(i, (i + 1) % count) for i in range(count)])]
    pallas_call x0 -> x1, Pallas kernels: none -> 62 us  [local(): pl.pallas_call(functools.partial(kernel, sizes, chunks), out_shape=jax.Sh...]
    ppermute x42 -> x0, starting transfers between devices: 39.7 us -> none  [the longest x21 21.9 us: extended(): lax.ppermute(head, axis, [((i + 1) % count, i) for i in range(count)])]
    div x3 -> x0, other arithmetic: 17 us -> none  [the longest x1 16.7 us: local(): first_wide = (first_image - middle * inner) / spread]
    concatenate x8 -> x0, other arithmetic: 8.22 us -> none  [extended(): jnp.concatenate([lax.ppermute(tail, axis, [(i, (i + 1) % count) for i in...]
    sub x2 -> x0, other arithmetic: 7.81 us -> none  [the longest x1 7.46 us: local(): 2.0 * (second_image - middle * first_order) / spread - orbitals]
    slice x13 -> x0, local copies, waits for them, and re-layouts: 7.74 us -> none  [the longest x11 4.29 us: extended(): lax.slice_in_dim(cells, cells.shape[dim] - width, cells.shape[dim], axis=...]
    ppermute x4 -> x0, local copies, waits for them, and re-layouts: 6.26 us -> none  [the longest x2 3.16 us: extended(): lax.ppermute(tail, axis, [(i, (i + 1) % count) for i in range(count)])]
  transfers between devices with their start and end apart: 42 -> 0, of which waited for: 33 -> 0; matrix products, arithmetic and copies ran while one was open for 8% -> 0% of each run, Pallas kernels for 0% -> 0%
where the time goes in v1:
time: 67.2 us; the launch traced here: 67 us
  Pallas kernels  62 us (92%)
  local copies, waits for them, and re-layouts  4.98 us (7%)
    pallas_call x1, Pallas kernels, local(): pl.pallas_call(functools.partial(kernel, sizes, chunks), out_shape=jax.Sh...  62 us
    unnamed x9, local copies, waits for them, and re-layouts  4.98 us

profile of v1, /device:TPU:0, one launch (start us, length us, event | category | flops | bytes accessed | tf_op | source)
XLA Modules:
  0.0 67.0 jit_solution(3891496896635562321)
XLA Ops:
  0.0 0.0 copy-start
  0.0 1.6 %copy-done = f32[64,8,8,128]{3,2,1,0:T(8,128)S(1)} copy-done((f32[64,8,8,128]{3,2,1,0:T(8,128)S(1)}, f32[64,8,8,128]{3,2,1,0:T(8,128)}, u32[]{:S(2)}) %copy-start) | copy-done | bytes 2097176
  1.6 0.0 copy-start.1
  1.6 0.8 %copy-done.1 = f32[8,8,128]{2,1,0:T(8,128)S(1)} copy-done((f32[8,8,128]{2,1,0:T(8,128)S(1)}, f32[8,8,128]{2,1,0:T(8,128)}, u32[]{:S(2)}) %copy-start.1) | copy-done | bytes 32792
  2.4 0.0 copy-start.2
  2.4 0.7 copy-done.2
  3.0 0.0 copy-start.3
  3.0 0.7 copy-done.3
  3.7 62.0 %shard_map.46 = f32[64,8,8,128]{3,2,1,0:T(8,128)S(1)} custom-call(f32[64]{0:T(128)S(1)} %copy-done.2, f32[64]{0:T(128)S(1)} %copy-done.3, f32[8,8,128]{2,1,0:T(8,128)S(1)} %copy-done.1, f32[64,8,8,128]{3,2,1,0:T(8,128)S(1)} %copy-done), custom_call_target="tpu_custom_call" | custom-call | tf_op jit(solution)/shard_map/pallas_call | solution.py:352
  65.7 1.3 %copy.6 = f32[64,8,8,128]{3,2,1,0:T(8,128)} copy(f32[64,8,8,128]{3,2,1,0:T(8,128)S(1)} %shard_map.46) | data formatting | bytes 4194304
Async XLA Ops:
  0.0 1.6 %copy-start = (f32[64,8,8,128]{3,2,1,0:T(8,128)S(1)}, f32[64,8,8,128]{3,2,1,0:T(8,128)}, u32[]{:S(2)}) copy-start(f32[64,8,8,128]{3,2,1,0:T(8,128)} %orbitals.1) | copy-start | bytes 6291460
  1.6 0.8 %copy-start.1 = (f32[8,8,128]{2,1,0:T(8,128)S(1)}, f32[8,8,128]{2,1,0:T(8,128)}, u32[]{:S(2)}) copy-start(f32[8,8,128]{2,1,0:T(8,128)} %pot.1) | copy-start | bytes 98308
  2.4 0.7 copy-start.2
  3.0 0.7 copy-start.3

commit v2 on v1

--- a/solution.py
+++ b/solution.py
@@ -13,10 +13,12 @@
 ORB, FIRST, LEV_A, LEV_B, TWO_A, TWO_B, TWO_C = range(7)
 
 
-def kernel(sizes, chunks, centre, half_width, pot, orbitals, out, *scratch):
+def kernel(sizes, chunks, centre_in, half_width_in, pot_in, orbitals, out, *scratch):
     ext = scratch[0:7]
     second, zsend, zrecv, band_a, band_i, pot_b, d1_b, r1_b, r2_b = scratch[7:16]
     load_sem, store_sem, send_sem, recv_sem = scratch[16:20]
+    centre, half_width, pot, small_sem = scratch[20:24]
+    packed_out, packed_in = scratch[24:29], scratch[29:34]
     bands, nx, ny, nz = second.shape[2], second.shape[0], second.shape[1], second.shape[3]
     width = bands // chunks
     groups = width // 8
@@ -33,6 +35,13 @@
     if two_sided:
         peers.append(near["gz"][0])
 
+    smalls = [
+        pltpu.make_async_copy(src, dst, small_sem.at[j])
+        for j, (src, dst) in enumerate(
+            [(centre_in, centre), (half_width_in, half_width), (pot_in, pot)]
+        )
+    ]
+
     def loads(k):
         rows = pl.ds(pl.multiple_of(k * width, 8), width)
 
@@ -46,6 +55,8 @@
         lax.fori_loop(0, nx, line, 0)
 
     lax.fori_loop(0, chunks, lambda k, c: (loads(k), c)[1], 0)
+    for small in smalls:
+        small.start()
 
     barrier = pltpu.get_barrier_semaphore()
     for peer in peers:
@@ -56,13 +67,24 @@
         e = ext[p]
         rows = pl.ds(pl.multiple_of(k * width, 8), width)
         ys, xs = pl.ds(1, my), pl.ds(1, mx)
-        moves = [
-            (e.at[1, ys, rows], e.at[mx + 1, ys, rows], near["gx"][0]),
-            (e.at[mx, ys, rows], e.at[0, ys, rows], near["gx"][1]),
-            (e.at[xs, 1, rows], e.at[xs, my + 1, rows], near["gy"][0]),
-            (e.at[xs, my, rows], e.at[xs, 0, rows], near["gy"][1]),
-            (zsend.at[p, rows], zrecv.at[p, 0, rows], near["gz"][1]),
-        ]
+        if p in (ORB, FIRST):
+            moves = [
+                (e.at[xs, 1, rows], e.at[xs, my + 1, rows], near["gy"][0]),
+                (e.at[xs, my, rows], e.at[xs, 0, rows], near["gy"][1]),
+                (e.at[1, ys, rows], e.at[mx + 1, ys, rows], near["gx"][0]),
+                (e.at[mx, ys, rows], e.at[0, ys, rows], near["gx"][1]),
+            ]
+        else:
+            share = width if p in (LEV_A, LEV_B) else width // 2
+            part = pl.ds(pl.multiple_of(k * share, 8), share)
+            sent, got = packed_out[p - LEV_A], packed_in[p - LEV_A]
+            moves = [
+                (sent.at[j, :, part], got.at[j, :, part], near[axis][side])
+                for j, (axis, side) in enumerate(
+                    [("gy", 0), ("gy", 1), ("gx", 0), ("gx", 1)]
+                )
+            ]
+        moves.append((zsend.at[p, rows], zrecv.at[p, 0, rows], near["gz"][1]))
         if two_sided:
             moves.append((zsend.at[p, rows], zrecv.at[p, 1, rows], near["gz"][0]))
         return [
@@ -77,13 +99,57 @@
             for j, (src, dst, to) in enumerate(moves)
         ]
 
+    def items(p, k):
+        mx, my, w = dims[p]
+        base = k * width
+        if w == 2:
+            for i in range(width // 8):
+                at = pl.ds(pl.multiple_of(base + 8 * i, 8), 8)
+                for pair in range(mx // 2):
+                    yield pair, at, [(2 * pair, at), (2 * pair + 1, at)]
+        else:
+            for i in range(width // 16):
+                rows = [pl.ds(pl.multiple_of(base + 16 * i + 8 * h, 8), 8) for h in (0, 1)]
+                at = pl.ds(pl.multiple_of(k * (width // 2) + 8 * i, 8), 8)
+                for pair in range(mx // 2):
+                    yield pair, at, [(2 * pair + c, r) for r in rows for c in (0, 1)]
+
+    def face_cell(p, j, cell, halo):
+        mx, my, _ = dims[p]
+        if j < 2:
+            return (cell + 1, ((my + 1, 0) if halo else (1, my))[j])
+        return (((mx + 1, 0) if halo else (1, mx))[j - 2], cell + 1)
+
     def send(p, k):
+        if p not in (ORB, FIRST):
+            w = dims[p][2]
+            for pair, at, parts in items(p, k):
+                for j in range(4):
+                    acc = None
+                    for spot, (cell, r) in enumerate(parts):
+                        cx, cy = face_cell(p, j, cell, False)
+                        v = ext[p][cx, cy, r]
+                        acc = v if acc is None else jnp.where(lax.rem(lane, w) == spot, v, acc)
+                    packed_out[p - LEV_A][j, pair, at] = acc
         for copy in copies(p, k):
             copy.start()
 
     def receive(p, k):
         for copy in copies(p, k):
             copy.wait_recv()
+        if p not in (ORB, FIRST):
+            w = dims[p][2]
+            for pair, at, parts in items(p, k):
+                for j in range(4):
+                    got = packed_in[p - LEV_A][j, pair, at]
+                    for spot, (cell, r) in enumerate(parts):
+                        cx, cy = face_cell(p, j, cell, True)
+                        v = jnp.where(lax.rem(lane, w) == spot, got, 0.0)
+                        reach = 1
+                        while reach < w:
+                            v = v + roll(v, -reach if spot & reach else reach)
+                            reach *= 2
+                        ext[p][cx, cy, r] = v
 
     def roll(v, shift):
         return pltpu.roll(v, shift % nz, v.ndim - 1)
@@ -134,20 +200,42 @@
         def one(k, carry):
             if p_in is not None:
                 receive(p_in, k)
-            for gg in range(groups) if groups == 1 else [None]:
-                if gg is None:
-                    def inner(i, c):
-                        body(pl.ds(pl.multiple_of(k * width + i * 8, 8), 8))
-                        return c
-                    lax.fori_loop(0, groups, inner, 0)
-                else:
-                    body(pl.ds(pl.multiple_of(k * width, 8), 8))
+
+            def inner(i, c):
+                body(pl.ds(pl.multiple_of(k * width + i * 8, 8), 8))
+                return c
+
+            lax.fori_loop(0, groups, inner, 0)
             if p_out is not None:
                 send(p_out, k)
             return carry
 
         lax.fori_loop(0, chunks, one, 0)
 
+    pl.semaphore_wait(barrier, len(peers))
+
+    def start(k, carry):
+        rows = pl.ds(pl.multiple_of(k * width, 8), width)
+        whole = ext[ORB].at[pl.ds(1, nx), pl.ds(1, ny), rows]
+        pltpu.make_async_copy(whole, whole, load_sem.at[k]).wait()
+
+        moves = copies(ORB, k)
+        for copy in moves[:4]:
+            copy.start()
+
+        def inner(i, c):
+            pack_store(ORB, pl.ds(pl.multiple_of(k * width + i * 8, 8), 8))
+            return c
+
+        lax.fori_loop(0, groups, inner, 0)
+        for copy in moves[4:]:
+            copy.start()
+        return carry
+
+    lax.fori_loop(0, chunks, start, 0)
+
+    for small in smalls:
+        small.wait()
     for g in range(bands // 8):
         m = jnp.zeros((8, nz), jnp.float32)
         s = jnp.ones((8, nz), jnp.float32)
@@ -174,23 +262,6 @@
                     r1_b[x, y] = jacobi_weight / d1
             r2_b[qx, qy] = jacobi_weight / (0.1875 + 0.125 * pair_sum(quad, 2) + shift_mass)
 
-    pl.semaphore_wait(barrier, len(peers))
-
-    def start(k, carry):
-        rows = pl.ds(pl.multiple_of(k * width, 8), width)
-        whole = ext[ORB].at[pl.ds(1, nx), pl.ds(1, ny), rows]
-        pltpu.make_async_copy(whole, whole, load_sem.at[k]).wait()
-
-        def inner(i, c):
-            pack_store(ORB, pl.ds(pl.multiple_of(k * width + i * 8, 8), 8))
-            return c
-
-        lax.fori_loop(0, groups, inner, 0)
-        send(ORB, k)
-        return carry
-
-    lax.fori_loop(0, chunks, start, 0)
-
     def step_first(sl):
         got = edges(ORB, sl)
         a, i = band_a[sl], band_i[sl]
@@ -348,20 +419,22 @@
         pltpu.SemaphoreType.DMA((chunks,)),
         pltpu.SemaphoreType.DMA((7, chunks, 6)),
         pltpu.SemaphoreType.DMA((7, chunks, 6)),
+        pltpu.SMEM((bands,), jnp.float32),
+        pltpu.SMEM((bands,), jnp.float32),
+        f32(nx, ny, nz),
+        pltpu.SemaphoreType.DMA((3,)),
     ]
+    for _ in range(2):
+        scratch += [f32(4, max(nx, ny) // 4, bands, nz)] * 2
+        scratch += [f32(4, max(nx, ny) // 8, bands // 2, nz)] * 3
     return pl.pallas_call(
         functools.partial(kernel, sizes, chunks),
         out_shape=jax.ShapeDtypeStruct(orbitals.shape, jnp.float32),
-        in_specs=[
-            pl.BlockSpec(memory_space=pltpu.SMEM),
-            pl.BlockSpec(memory_space=pltpu.SMEM),
-            pl.BlockSpec(memory_space=pltpu.VMEM),
-            pl.BlockSpec(memory_space=pl.ANY),
-        ],
+        in_specs=[pl.BlockSpec(memory_space=pltpu.HBM)] * 4,
         out_specs=pl.BlockSpec(memory_space=pl.ANY),
         scratch_shapes=scratch,
         compiler_params=pltpu.CompilerParams(
-            collective_id=0, has_side_effects=True, vmem_limit_bytes=48 * 1024 * 1024
+            collective_id=0, has_side_effects=True, vmem_limit_bytes=67_043_328
         ),
     )(centre, half_width, potential, orbitals)
 

time: 67.2 us -> 60.4 us (0.90)
  Pallas kernels: 62 us -> 57.1 us
  local copies, waits for them, and re-layouts: 4.98 us -> 3.16 us
    pallas_call x1, Pallas kernels: 62 us -> 57.1 us  [local(): pl.pallas_call(functools.partial(kernel, sizes, chunks), out_shape=jax.Sh...]
    unnamed x9 -> x1, local copies, waits for them, and re-layouts: 4.98 us -> 3.16 us
where the time goes in v2:
time: 60.4 us; the launch traced here: 60.3 us
  Pallas kernels  57.1 us (95%)
  local copies, waits for them, and re-layouts  3.16 us (5%)
    pallas_call x1, Pallas kernels, local(): pl.pallas_call(functools.partial(kernel, sizes, chunks), out_shape=jax.Sh...  57.1 us
    unnamed x1, local copies, waits for them, and re-layouts  3.16 us

profile of v2, /device:TPU:0, one launch (start us, length us, event | category | flops | bytes accessed | tf_op | source)
XLA Modules:
  0.0 60.3 jit_solution(5919374624572382188)
XLA Ops:
  0.0 57.1 %shard_map.46 = f32[64,8,8,128]{3,2,1,0:T(8,128)} custom-call(f32[64]{0:T(128)} %centre_in.1, f32[64]{0:T(128)} %half_width_in.1, f32[8,8,128]{2,1,0:T(8,128)} %pot_in.1, f32[64,8,8,128]{3,2,1,0:T(8,128)} %orbitals.1), custom_call_target="tpu_custom_call" | custom-call | tf_op jit(solution)/shard_map/pallas_call | solution.py:430
  57.1 3.2 %copy.6 = f32[64,8,8,128]{3,2,1,0:T(8,128)} copy(f32[64,8,8,128]{3,2,1,0:T(8,128)} %shard_map.46) | data formatting | bytes 4194304

commit v3 on v2

--- a/solution.py
+++ b/solution.py
@@ -434,9 +434,9 @@
         out_specs=pl.BlockSpec(memory_space=pl.ANY),
         scratch_shapes=scratch,
         compiler_params=pltpu.CompilerParams(
-            collective_id=0, has_side_effects=True, vmem_limit_bytes=67_043_328
+            collective_id=0, has_side_effects=True, vmem_limit_bytes=48 * 1024 * 1024
         ),
-    )(centre, half_width, potential, orbitals)
+    )(*(pltpu.with_memory_space_constraint(v, pltpu.HBM) for v in (centre, half_width, potential, orbitals)))
 
 
 def solution(mesh):

time: 60.4 us -> 58.8 us (0.974)
  local copies, waits for them, and re-layouts: 3.16 us -> 1.32 us
    unnamed x1, local copies, waits for them, and re-layouts: 3.16 us -> 1.32 us
where the time goes in v3:
time: 58.8 us; the launch traced here: 58.7 us
  Pallas kernels  57.3 us (97%)
  local copies, waits for them, and re-layouts  1.32 us (2%)
    pallas_call x1, Pallas kernels, local(): pl.pallas_call(functools.partial(kernel, sizes, chunks), out_shape=jax.Sh...  57.3 us
    unnamed x1, local copies, waits for them, and re-layouts  1.32 us

profile of v3, /device:TPU:0, one launch (start us, length us, event | category | flops | bytes accessed | tf_op | source)
XLA Modules:
  0.0 58.7 jit_solution(6878708006087185749)
XLA Ops:
  0.0 57.3 %shard_map.46 = f32[64,8,8,128]{3,2,1,0:T(8,128)S(1)} custom-call(f32[64]{0:T(128)} %centre_in.1, f32[64]{0:T(128)} %half_width_in.1, f32[8,8,128]{2,1,0:T(8,128)} %pot_in.1, f32[64,8,8,128]{3,2,1,0:T(8,128)} %orbitals.1), custom_call_target="tpu_custom_call" | custom-call | tf_op jit(solution)/shard_map/pallas_call | solution.py:430
  57.3 1.3 %copy.6 = f32[64,8,8,128]{3,2,1,0:T(8,128)} copy(f32[64,8,8,128]{3,2,1,0:T(8,128)S(1)} %shard_map.46) | data formatting | bytes 4194304

commit v4 on v3

--- a/solution.py
+++ b/solution.py
@@ -129,7 +129,7 @@
                     for spot, (cell, r) in enumerate(parts):
                         cx, cy = face_cell(p, j, cell, False)
                         v = ext[p][cx, cy, r]
-                        acc = v if acc is None else jnp.where(lax.rem(lane, w) == spot, v, acc)
+                        acc = v if acc is None else jnp.where((lane & (w - 1)) == spot, v, acc)
                     packed_out[p - LEV_A][j, pair, at] = acc
         for copy in copies(p, k):
             copy.start()
@@ -144,7 +144,7 @@
                     got = packed_in[p - LEV_A][j, pair, at]
                     for spot, (cell, r) in enumerate(parts):
                         cx, cy = face_cell(p, j, cell, True)
-                        v = jnp.where(lax.rem(lane, w) == spot, got, 0.0)
+                        v = jnp.where((lane & (w - 1)) == spot, got, 0.0)
                         reach = 1
                         while reach < w:
                             v = v + roll(v, -reach if spot & reach else reach)
@@ -171,7 +171,7 @@
         w = dims[p][2]
         got = zrecv[p, 0, sl]
         if two_sided:
-            got = jnp.where(lax.rem(lane, 2 * w) < w, got, zrecv[p, 1, sl])
+            got = jnp.where((lane & (2 * w - 1)) < w, got, zrecv[p, 1, sl])
         return got
 
     def edge_at(p, got, x, y):
@@ -193,7 +193,7 @@
         return c, total + along_z(c, h, w)
 
     def pair_sum(v, w):
-        even = lax.rem(lane, 2 * w) < w
+        even = (lane & (2 * w - 1)) < w
         return v + jnp.where(even, roll(v, -w), roll(v, w))
 
     def each(body, p_in, p_out):

time: 58.8 us -> 58.8 us (level)
  no operation moved by 1% of the time
where the time goes in v4:
time: 58.8 us; the launch traced here: 58.7 us
  Pallas kernels  57.3 us (97%)
  local copies, waits for them, and re-layouts  1.32 us (2%)
    pallas_call x1, Pallas kernels, local(): pl.pallas_call(functools.partial(kernel, sizes, chunks), out_shape=jax.Sh...  57.3 us
    unnamed x1, local copies, waits for them, and re-layouts  1.32 us

profile of v4, /device:TPU:0, one launch (start us, length us, event | category | flops | bytes accessed | tf_op | source)
XLA Modules:
  0.0 58.7 jit_solution(6878708006087185749)
XLA Ops:
  0.0 57.3 %shard_map.46 = f32[64,8,8,128]{3,2,1,0:T(8,128)S(1)} custom-call(f32[64]{0:T(128)} %centre_in.1, f32[64]{0:T(128)} %half_width_in.1, f32[8,8,128]{2,1,0:T(8,128)} %pot_in.1, f32[64,8,8,128]{3,2,1,0:T(8,128)} %orbitals.1), custom_call_target="tpu_custom_call" | custom-call | tf_op jit(solution)/shard_map/pallas_call | solution.py:430
  57.3 1.3 %copy.6 = f32[64,8,8,128]{3,2,1,0:T(8,128)} copy(f32[64,8,8,128]{3,2,1,0:T(8,128)S(1)} %shard_map.46) | data formatting | bytes 4194304
